TPU v7x, 32 devices: a whole 2x2x4 slice. The times are simulated.
32 devices in a mesh: vx: 4 (over y, x), vy: 8 (over z, core).
Axes of the slice: x: 2, y: 2, z: 4, core: 2. Of those that a mesh axis runs over, the one named last changes fastest.
Arguments:
- tokens: bfloat16 [96, 1, 256, 1024], P(('vx', 'vy')), may hold values from -256 to 256
- var_embed: bfloat16 [91, 1024], replicated, may hold values from -2 to 2
- query: bfloat16 [1024], replicated, may hold values from -6 to 6
- key_weight: bfloat16 [1024, 1024], P('vy'), may hold values from -1 to 1
- value_weight: bfloat16 [1024, 1024], P('vy'), may hold values from -0.1875 to 0.1875
- out_weight: bfloat16 [1024, 1024], P('vy'), may hold values from -0.1875 to 0.1875
- var_slot: int32 [91], replicated, may hold values from 0 to 95, as said below
Outputs:
- aggregated: bfloat16 [1, 256, 1024], P(None, ('vx', 'vy'))
Inputs may be any that keep to these rules, and one draw needn't show every extreme that they name: `var_slot`: distinct slot numbers; at least one device's slot holds a variable.
All inputs are finite; a program needn't handle non-finite values.
Results may differ from a plain program's by a relative error of at most 0.0096.
Values may be sent and summed in bfloat16 or wider, within the bound.
A program may use at most 64 MiB of HBM per device.

v0:
```python
import math
import jax
import jax.numpy as jnp
from jax import lax
from jax.sharding import PartitionSpec as P

HEADS = 16


def attend(keys, values, query_matrix, scale, heads):
    scores = (
        jnp.einsum("vbpd,dh->vbph", keys, query_matrix, preferred_element_type=jnp.float32) * scale
    )
    highest = jnp.max(scores, axis=0, keepdims=True)
    exponent = jnp.exp(scores - highest)
    weights = (exponent / jnp.sum(exponent, axis=0, keepdims=True)).astype(jnp.bfloat16)
    shaped = values.reshape(values.shape[:3] + (heads, values.shape[3] // heads))
    context = jnp.einsum("vbph,vbphe->bphe", weights, shaped, preferred_element_type=jnp.float32)
    return context.astype(jnp.bfloat16).reshape(values.shape[1:])


def shards(tokens, var_embed, query, key_weight, value_weight, out_weight, var_slot):
    slot_dev, batch, patches, width = tokens.shape
    heads = HEADS
    scale = 1.0 / math.sqrt(width // heads)
    count_y = lax.axis_size("vy")
    position = lax.axis_index("vx") * count_y + lax.axis_index("vy")
    local_slots = position * slot_dev + jnp.arange(slot_dev, dtype=jnp.int32)
    slot_match = (local_slots[:, None] == var_slot[None, :]).astype(jnp.bfloat16)
    embed_rows = jnp.dot(slot_match, var_embed, preferred_element_type=jnp.float32)
    mixed = (tokens.astype(jnp.float32) + embed_rows[:, None, None, :]).astype(jnp.bfloat16)
    key_full, value_full = (
        lax.all_gather(key_weight, "vy", axis=0, tiled=True),
        lax.all_gather(value_weight, "vy", axis=0, tiled=True),
    )
    stacked = jnp.stack((key_full, value_full))
    head_of = jnp.arange(width, dtype=jnp.int32) // (width // heads)
    query_matrix = jnp.where(
        head_of[:, None] == jnp.arange(heads, dtype=jnp.int32)[None, :],
        query[:, None],
        jnp.zeros((), jnp.bfloat16),
    )
    outgoing = mixed[None]
    selected = jnp.take(
        lax.all_to_all(outgoing, ("vx", "vy"), split_axis=3, concat_axis=1, tiled=True),
        var_slot,
        axis=1,
    )
    projected = jnp.einsum(
        "vbpd,cde->cvbpe", selected[0], stacked, preferred_element_type=jnp.float32
    ).astype(jnp.bfloat16)
    keys = projected[0]
    values = projected[1]
    context = attend(keys, values, query_matrix, scale, heads)
    flattened = context.reshape(-1, width)
    result = jnp.dot(
        flattened,
        lax.all_gather(out_weight, "vy", axis=0, tiled=True),
        preferred_element_type=jnp.float32,
    )
    return result.astype(jnp.bfloat16).reshape(batch, -1, width)


def solution(mesh):
    placed = (
        P(("vx", "vy"), None, None, None),
        P(),
        P(),
        P("vy", None),
        P("vy", None),
        P("vy", None),
        P(),
    )
    return jax.shard_map(
        shards, mesh=mesh, in_specs=placed, out_specs=P(None, ("vx", "vy"), None), check_vma=False
    )
```

profile of v0, /device:TPU:0, one launch (start us, length us, event | category | flops | bytes accessed | tf_op | source)
XLA Modules:
  0.0 141.9 jit_solution(14651676802304566514)
XLA Ops:
  6.5 0.0 copy-start
  6.5 0.0 all-gather.4.cloned.1.call-start
  6.5 0.7 all-gather.4.cloned.1.call-update
  7.3 0.0 all-gather.6.cloned.1.call-start
  7.3 0.7 all-gather.6.cloned.1.call-update
  8.0 0.0 copy-done
  8.0 0.9 fusion.27
  8.9 4.1 %fusion.5 = bf16[1,3,1,256,1024]{4,1,2,0,3:T(4,128)(2,1)} fusion(bf16[3,1,256,1024]{3,2,1,0:T(8,128)(2,1)} %param.7, f32[3,1024]{1,0:T(4,128)S(1)} %fusion.27), kind=kLoop, calls=%fused_computation.9 | loop fusion | flops 2359296 | bytes 3158016 | tf_op jit(solution)/shard_map/broadcast_in_dim | solution.py:43
  13.0 7.3 %all-to-all-start = ((bf16[1,3,1,256,1024]{4,1,2,0,3:T(4,128)(2,1)}), bf16[1,3,1,256,1024]{4,1,2,0,3:T(4,128)(2,1)S(1)}, u32[]{:S(2)}, u32[]{:S(2)}) async-start(bf16[1,3,1,256,1024]{4,1,2,0,3:T(4,128)(2,1)} %fusion.5), calls=%async_computation | async-start | bytes 4194304 | tf_op jit(solution)/shard_map/all_to_all | solution.py:45
  20.3 0.0 all-gather.8.cloned.1.call-start
  20.4 0.7 all-gather.8.cloned.1.call-update
  21.1 0.0 copy-done.4
  21.1 78.7 %all-to-all-done = bf16[1,3,1,256,1024]{4,1,2,0,3:T(4,128)(2,1)S(1)} async-done(((bf16[1,3,1,256,1024]{4,1,2,0,3:T(4,128)(2,1)}), bf16[1,3,1,256,1024]{4,1,2,0,3:T(4,128)(2,1)S(1)}, u32[]{:S(2)}, u32[]{:S(2)}) %all-to-all-start) | async-done | bytes 1572896 | tf_op jit(solution)/shard_map/all_to_all | solution.py:45
  99.8 0.6 copy.32
  100.4 0.1 copy.18
  100.5 0.7 gather_fusion
  101.3 0.2 broadcast_select_fusion
  101.5 0.0 all-gather.4.cloned.1.call-done
  101.5 1.6 %all-gather.6.cloned.1.call-done = bf16[1024,1024]{1,0:T(8,128)(2,1)} async-done(((bf16[128,1024]{1,0:T(8,128)(2,1)}), bf16[1024,1024]{1,0:T(8,128)(2,1)}) %all-gather.6.cloned.1.call-update) | async-done | bytes 2097168 | tf_op jit(solution)/shard_map/all_gather | solution.py:34
  103.1 6.0 %convert_bitcast_fusion = bf16[2,91,1,8,1024]{4,1,3,0,2:T(8,128)(2,1)S(1)} fusion(bf16[1,1024,1024]{2,1,0:T(8,128)(2,1)} %bitcast.56, bf16[1,1024,1024]{2,1,0:T(8,128)(2,1)} %bitcast.55, bf16[91,8,1024]{2,1,0:T(8,128)(2,1)S(1)} %broadcast_select_fusion), kind=kOutput, calls=%fused_computation.8 | convolution fusion | flops 3063332864 | bytes 8667136 | tf_op jit(solution)/shard_map/vbpd,cde->cvbpe/dot_general | solution.py:49
  109.1 0.0 copy-start.2
  109.1 1.7 %copy-done.2 = bf16[2,91,1,8,1024]{4,1,3,0,2:T(8,128)(2,1)} copy-done((bf16[2,91,1,8,1024]{4,1,3,0,2:T(8,128)(2,1)}, bf16[2,91,1,8,1024]{4,1,3,0,2:T(8,128)(2,1)S(1)}, u32[]{:S(2)}) %copy-start.2) | copy-done | bytes 2981912
  110.8 0.1 slice.11
  110.9 0.0 copy-start.3
  110.9 2.5 %copy.20 = bf16[1,91,1,8,1024]{1,4,3,2,0:T(8,128)(2,1)} copy(bf16[1,91,1,8,1024]{4,1,3,0,2:T(8,128)(2,1)S(1)} %slice.11) | data formatting | bytes 2981888 | tf_op jit(solution)/shard_map/slice | solution.py:53
  113.4 0.0 copy-done.3
  113.5 2.3 %fusion.14 = bf16[91,8,16,1]{0,2,1,3:T(8,128)(2,1)S(1)} fusion(bf16[2,91,1,8,1024]{4,1,3,0,2:T(8,128)(2,1)} %copy-done.2, s32[1024]{0:T(1024)S(1)} %add_select_fusion, bf16[1024]{0:T(1024)(128)(2,1)S(1)} %copy-done.3), kind=kOutput, calls=%fused_computation.21 | convolution fusion | flops 23934900 | bytes 1602304 | tf_op jit(solution)/shard_map/div | solution.py:16
  115.8 0.0 copy-done.1
  115.8 1.2 fusion.16
  117.0 0.1 reshape_reshape.3
  117.1 15.7 %all-gather.8.cloned.1.call-done = bf16[1024,1024]{1,0:T(8,128)(2,1)} async-done(((bf16[128,1024]{1,0:T(8,128)(2,1)}), bf16[1024,1024]{1,0:T(8,128)(2,1)}) %all-gather.8.cloned.1.call-update) | async-done | bytes 2097168 | tf_op jit(solution)/shard_map/all_gather | solution.py:58
  132.7 2.6 %fusion.15 = bf16[1,8,1024]{2,1,0:T(8,128)(2,1)} fusion(bf16[8,1024]{1,0:T(8,128)(2,1)S(1)} %reshape_reshape.3, bf16[1024,1024]{1,0:T(8,128)(2,1)} %all-gather.8.cloned.1.call-done), kind=kOutput, calls=%fused_computation.23 | convolution fusion | flops 16785408 | bytes 2129920 | tf_op jit(solution)/shard_map/dot_general | solution.py:56
  (8 shorter events, 0.0 us)
Async XLA Ops:
  6.5 1.5 %copy-start = (bf16[91,1024]{1,0:T(8,128)(2,1)S(1)}, bf16[91,1024]{1,0:T(8,128)(2,1)}, u32[]{:S(2)}) copy-start(bf16[91,1024]{1,0:T(8,128)(2,1)} %param.8) | copy-start | bytes 559108
  6.5 95.0 %all-gather.4.cloned.1.call-start = ((), (), s32[]{:S(2)}) async-start(), calls=%async_computation.1 | async-start | bytes 2359296 | tf_op jit(solution)/shard_map/all_gather | solution.py:33
  7.3 95.8 %all-gather.6.cloned.1.call-start = ((), (), s32[]{:S(2)}) async-start(), calls=%async_computation.2 | async-start | bytes 2359296 | tf_op jit(solution)/shard_map/all_gather | solution.py:34
  13.0 8.1 %copy-start.4 = (s32[91]{0:T(128)S(1)}, s32[91]{0:T(128)}, u32[]{:S(2)}) copy-start(s32[91]{0:T(128)} %param.13) | copy-start | bytes 1096
  13.0 86.8 %all-to-all-start = ((bf16[1,3,1,256,1024]{4,1,2,0,3:T(4,128)(2,1)}), bf16[1,3,1,256,1024]{4,1,2,0,3:T(4,128)(2,1)S(1)}, u32[]{:S(2)}, u32[]{:S(2)}) async-start(bf16[1,3,1,256,1024]{4,1,2,0,3:T(4,128)(2,1)} %fusion.5), calls=%async_computation | async-start | bytes 4194304 | tf_op jit(solution)/shard_map/all_to_all | solution.py:45
  20.3 112.4 %all-gather.8.cloned.1.call-start = ((), (), s32[]{:S(2)}) async-start(), calls=%async_computation.3 | async-start | bytes 2359296 | tf_op jit(solution)/shard_map/all_gather | solution.py:58
  109.1 1.7 %copy-start.2 = (bf16[2,91,1,8,1024]{4,1,3,0,2:T(8,128)(2,1)}, bf16[2,91,1,8,1024]{4,1,3,0,2:T(8,128)(2,1)S(1)}, u32[]{:S(2)}) copy-start(bf16[2,91,1,8,1024]{4,1,3,0,2:T(8,128)(2,1)S(1)} %convert_bitcast_fusion) | copy-start | bytes 8945668
  110.9 2.5 %copy-start.3 = (bf16[1024]{0:T(1024)(128)(2,1)S(1)}, bf16[1024]{0:T(1024)(128)(2,1)}, u32[]{:S(2)}) copy-start(bf16[1024]{0:T(1024)(128)(2,1)} %param.9) | copy-start | bytes 6148
  113.5 2.3 %copy-start.1 = (bf16[1,91,1,8,1024]{1,4,3,2,0:T(8,128)(2,1)S(1)}, bf16[1,91,1,8,1024]{1,4,3,2,0:T(8,128)(2,1)}, u32[]{:S(2)}) copy-start(bf16[1,91,1,8,1024]{1,4,3,2,0:T(8,128)(2,1)} %copy.20) | copy-start | bytes 4472836
Sparse Core Ops, SparseCore 0:
  8.9 49.8 all-gather.3
  60.4 42.6 all-gather.5
  104.7 28.0 all-gather.7
where the time goes:
time: 142 us
  waiting for transfers between devices  98 us (69%)
  between operations  13.3 us (9%)
  matrix products  13 us (9%)
  starting transfers between devices  7.41 us (5%)
  local copies, waits for them, and re-layouts  5.84 us (4%)
  other arithmetic  4.35 us (3%)
    all_to_all x1, waiting for transfers between devices, shards(): lax.all_to_all(outgoing, ('vx', 'vy'), split_axis=3, concat_axis=1, tiled...  78.7 us
    all_gather x1, waiting for transfers between devices, shards(): lax.all_gather(out_weight, 'vy', axis=0, tiled=True)  15.7 us
    all_to_all x1, starting transfers between devices, shards(): lax.all_to_all(outgoing, ('vx', 'vy'), split_axis=3, concat_axis=1, tiled...  7.33 us
    dot_general x1, matrix products, shards(): jnp.einsum('vbpd,cde->cvbpe', selected[0], stacked, preferred_element_typ...  6.04 us
    broadcast_in_dim x1, other arithmetic, shards(): outgoing = mixed[None]  4.11 us
  transfers between devices with their start and end apart: 4, of which 3 were waited for; matrix products, arithmetic and copies ran while one was open for 13% of the time, Pallas kernels for 0%

commit v1 on v0

--- a/solution.py
+++ b/solution.py
@@ -42,7 +42,15 @@
     )
     outgoing = mixed[None]
     selected = jnp.take(
-        lax.all_to_all(outgoing, ("vx", "vy"), split_axis=3, concat_axis=1, tiled=True),
+        jnp.concatenate(
+            lax.all_to_all(
+                jnp.stack(jnp.split(outgoing, lax.axis_size(("vx", "vy")), 3), axis=0),
+                axis_name=("vx", "vy"),
+                split_axis=0,
+                concat_axis=0,
+            ),
+            axis=1,
+        ),
         var_slot,
         axis=1,
     )

time: 142 us -> 129 us (0.908)
  waiting for transfers between devices: 98 us -> 67.4 us
  local copies, waits for them, and re-layouts: 5.84 us -> 25.3 us
  other arithmetic: 4.35 us -> 2.35 us
    all_to_all x1, waiting for transfers between devices: 78.7 us -> 54.8 us  [shards(): lax.all_to_all(jnp.stack(jnp.split(outgoing, lax.axis_size(('vx', 'vy')),...]
    unnamed x10 -> x41, local copies, waits for them, and re-layouts: 1.68 us -> 20.8 us
    all_gather x1, waiting for transfers between devices: 15.7 us -> 10.4 us  [shards(): lax.all_gather(out_weight, 'vy', axis=0, tiled=True)]
    div x1 -> x0, matrix products: 2.32 us -> none  [attend(): exponent / jnp.sum(exponent, axis=0, keepdims=True)]
    broadcast_in_dim x1, other arithmetic: 4.11 us -> 1.81 us  [shards(): outgoing = mixed[None]]
    dot_general x0 -> x1, matrix products: none -> 2.18 us  [attend(): jnp.einsum('vbpd,dh->vbph', keys, query_matrix, preferred_element_type=jn...]
    all_gather x1, waiting for transfers between devices: 1.58 us -> 0.02 us  [shards(): lax.all_gather(value_weight, 'vy', axis=0, tiled=True)]
  transfers between devices with their start and end apart: 4 -> 4, of which waited for: 3 -> 2; matrix products, arithmetic and copies ran while one was open for 13% -> 28% of each run, Pallas kernels for 0% -> 0%
where the time goes in v1:
time: 129 us
  waiting for transfers between devices  67.4 us (52%)
  local copies, waits for them, and re-layouts  25.3 us (20%)
  between operations  13.3 us (10%)
  matrix products  12.9 us (10%)
  starting transfers between devices  7.41 us (6%)
  other arithmetic  2.35 us (2%)
    all_to_all x1, waiting for transfers between devices, shards(): lax.all_to_all(jnp.stack(jnp.split(outgoing, lax.axis_size(('vx', 'vy')),...  54.8 us
    unnamed x41, local copies, waits for them, and re-layouts  20.8 us
    all_gather x1, waiting for transfers between devices, shards(): lax.all_gather(out_weight, 'vy', axis=0, tiled=True)  10.4 us
    all_to_all x1, starting transfers between devices, shards(): lax.all_to_all(jnp.stack(jnp.split(outgoing, lax.axis_size(('vx', 'vy')),...  7.33 us
    dot_general x1, matrix products, shards(): jnp.einsum('vbpd,cde->cvbpe', selected[0], stacked, preferred_element_typ...  6.08 us
    slice x2, local copies, waits for them, and re-layouts, shards(): values = projected[1]  2.6 us
    dot_general x1, matrix products, shards(): jnp.dot(flattened, lax.all_gather(out_weight, 'vy', axis=0, tiled=True),...  2.58 us
  transfers between devices with their start and end apart: 4, of which 2 were waited for; matrix products, arithmetic and copies ran while one was open for 28% of the time, Pallas kernels for 0%

profile of v1, /device:TPU:0, one launch (start us, length us, event | category | flops | bytes accessed | tf_op | source)
XLA Modules:
  0.0 128.6 jit_solution(13023215254570947546)
XLA Ops:
  6.5 0.7 all-gather.4.cloned.1.call-update
  7.3 0.7 all-gather.6.cloned.1.call-update
  8.0 0.9 fusion.19
  8.9 1.8 %fusion.3 = bf16[1,3,1,256,1024]{4,3,1,2,0:T(8,128)(2,1)S(1)} fusion(bf16[3,1,256,1024]{3,2,1,0:T(8,128)(2,1)} %param.7, f32[3,1024]{1,0:T(4,128)S(1)} %fusion.19), kind=kLoop, calls=%fused_computation.7 | loop fusion | flops 2359296 | bytes 3158016 | tf_op jit(solution)/shard_map/broadcast_in_dim | solution.py:43
  12.5 0.6 constant_dynamic-update-slice_fusion.28
  13.8 0.6 constant_dynamic-update-slice_fusion.26
  14.4 0.6 constant_dynamic-update-slice_fusion.25
  15.0 0.6 constant_dynamic-update-slice_fusion.24
  16.3 0.6 constant_dynamic-update-slice_fusion.22
  17.5 0.6 constant_dynamic-update-slice_fusion.20
  18.1 0.6 constant_dynamic-update-slice_fusion.19
  18.7 0.6 constant_dynamic-update-slice_fusion.18
  19.4 0.6 constant_dynamic-update-slice_fusion.17
  20.6 0.6 constant_dynamic-update-slice_fusion.15
  24.9 0.6 constant_dynamic-update-slice_fusion.8
  25.5 0.6 constant_dynamic-update-slice_fusion.7
  26.2 0.6 constant_dynamic-update-slice_fusion.6
  26.8 0.6 constant_dynamic-update-slice_fusion.5
  27.4 0.6 constant_dynamic-update-slice_fusion.4
  29.3 0.6 constant_dynamic-update-slice_fusion.1
  29.9 0.6 constant_dynamic-update-slice_fusion
  30.5 7.3 %all-to-all-start = ((bf16[32,1,3,1,8,1024]{5,4,2,3,1,0:T(8,128)(2,1)}), bf16[32,1,3,1,8,1024]{5,4,2,3,1,0:T(8,128)(2,1)S(1)}, u32[]{:S(2)}, u32[]{:S(2)}) async-start(bf16[32,1,3,1,8,1024]{5,4,2,3,1,0:T(8,128)(2,1)} %constant_dynamic-update-slice_fusion), calls=%async_computation | async-start | bytes 3145728 | tf_op jit(solution)/shard_map/all_to_all | solution.py:46
  37.9 0.7 all-gather.8.cloned.1.call-update
  38.7 54.8 %all-to-all-done = bf16[32,1,3,1,8,1024]{5,4,2,3,1,0:T(8,128)(2,1)S(1)} async-done(((bf16[32,1,3,1,8,1024]{5,4,2,3,1,0:T(8,128)(2,1)}), bf16[32,1,3,1,8,1024]{5,4,2,3,1,0:T(8,128)(2,1)S(1)}, u32[]{:S(2)}, u32[]{:S(2)}) %all-to-all-start) | async-done | bytes 1572896 | tf_op jit(solution)/shard_map/all_to_all | solution.py:46
  93.5 0.7 gather_fusion
  94.4 6.1 %convert_bitcast_fusion = bf16[2,91,1,8,1024]{4,1,3,0,2:T(8,128)(2,1)S(1)} fusion(bf16[1,1024,1024]{2,1,0:T(8,128)(2,1)} %bitcast.169, bf16[1,1024,1024]{2,1,0:T(8,128)(2,1)} %bitcast.168, bf16[91,8,1024]{2,1,0:T(8,128)(2,1)S(1)} %broadcast_select_fusion), kind=kOutput, calls=%fused_computation.5 | convolution fusion | flops 3063332864 | bytes 8667136 | tf_op jit(solution)/shard_map/vbpd,cde->cvbpe/dot_general | solution.py:57
  100.5 1.6 %copy-done.2 = bf16[2,91,1,8,1024]{4,1,3,0,2:T(8,128)(2,1)} copy-done((bf16[2,91,1,8,1024]{4,1,3,0,2:T(8,128)(2,1)}, bf16[2,91,1,8,1024]{4,1,3,0,2:T(8,128)(2,1)S(1)}, u32[]{:S(2)}) %copy-start.2) | copy-done | bytes 2981912
  102.3 2.5 %copy.11 = bf16[1,91,1,8,1024]{1,4,3,2,0:T(8,128)(2,1)} copy(bf16[1,91,1,8,1024]{4,1,3,0,2:T(8,128)(2,1)S(1)} %slice.11) | data formatting | bytes 2981888 | tf_op jit(solution)/shard_map/slice | solution.py:61
  104.8 2.2 %fusion.4 = f32[91,8,16]{0,2,1:T(8,128)S(1)} fusion(bf16[2,91,1,8,1024]{4,1,3,0,2:T(8,128)(2,1)} %copy-done.2, s32[1024]{0:T(1024)S(1)} %add_select_fusion, bf16[1024]{0:T(1024)(128)(2,1)S(1)} %copy-done.3), kind=kOutput, calls=%fused_computation.9 | convolution fusion | flops 23887872 | bytes 1625600 | tf_op jit(solution)/shard_map/vbpd,dh->vbph/dot_general | solution.py:12
  107.7 1.2 fusion.25
  109.0 10.4 %all-gather.8.cloned.1.call-done = bf16[1024,1024]{1,0:T(8,128)(2,1)} async-done(((bf16[128,1024]{1,0:T(8,128)(2,1)}), bf16[1024,1024]{1,0:T(8,128)(2,1)}) %all-gather.8.cloned.1.call-update) | async-done | bytes 2097168 | tf_op jit(solution)/shard_map/all_gather | solution.py:66
  119.4 2.6 %fusion.7 = bf16[1,8,1024]{2,1,0:T(8,128)(2,1)} fusion(bf16[8,1024]{1,0:T(8,128)(2,1)S(1)} %reshape_reshape.3, bf16[1024,1024]{1,0:T(8,128)(2,1)} %all-gather.8.cloned.1.call-done), kind=kOutput, calls=%fused_computation.14 | convolution fusion | flops 16785408 | bytes 2129920 | tf_op jit(solution)/shard_map/dot_general | solution.py:64
  (43 shorter events, 10.6 us)
Async XLA Ops:
  6.5 1.5 %copy-start = (bf16[91,1024]{1,0:T(8,128)(2,1)S(1)}, bf16[91,1024]{1,0:T(8,128)(2,1)}, u32[]{:S(2)}) copy-start(bf16[91,1024]{1,0:T(8,128)(2,1)} %param.8) | copy-start | bytes 559108
  6.5 87.9 %all-gather.4.cloned.1.call-start = ((), (), s32[]{:S(2)}) async-start(), calls=%async_computation.1 | async-start | bytes 2359296 | tf_op jit(solution)/shard_map/all_gather | solution.py:33
  7.3 87.2 %all-gather.6.cloned.1.call-start = ((), (), s32[]{:S(2)}) async-start(), calls=%async_computation.2 | async-start | bytes 2359296 | tf_op jit(solution)/shard_map/all_gather | solution.py:34
  30.5 8.1 %copy-start.4 = (s32[91]{0:T(128)S(1)}, s32[91]{0:T(128)}, u32[]{:S(2)}) copy-start(s32[91]{0:T(128)} %param.13) | copy-start | bytes 1096
  30.5 62.9 %all-to-all-start = ((bf16[32,1,3,1,8,1024]{5,4,2,3,1,0:T(8,128)(2,1)}), bf16[32,1,3,1,8,1024]{5,4,2,3,1,0:T(8,128)(2,1)S(1)}, u32[]{:S(2)}, u32[]{:S(2)}) async-start(bf16[32,1,3,1,8,1024]{5,4,2,3,1,0:T(8,128)(2,1)} %constant_dynamic-update-slice_fusion), calls=%async_computation | async-start | bytes 3145728 | tf_op jit(solution)/shard_map/all_to_all | solution.py:46
  37.9 81.6 %all-gather.8.cloned.1.call-start = ((), (), s32[]{:S(2)}) async-start(), calls=%async_computation.3 | async-start | bytes 2359296 | tf_op jit(solution)/shard_map/all_gather | solution.py:66
  100.5 1.6 %copy-start.2 = (bf16[2,91,1,8,1024]{4,1,3,0,2:T(8,128)(2,1)}, bf16[2,91,1,8,1024]{4,1,3,0,2:T(8,128)(2,1)S(1)}, u32[]{:S(2)}) copy-start(bf16[2,91,1,8,1024]{4,1,3,0,2:T(8,128)(2,1)S(1)} %convert_bitcast_fusion) | copy-start | bytes 8945668
  102.3 2.5 %copy-start.3 = (bf16[1024]{0:T(1024)(128)(2,1)S(1)}, bf16[1024]{0:T(1024)(128)(2,1)}, u32[]{:S(2)}) copy-start(bf16[1024]{0:T(1024)(128)(2,1)} %param.9) | copy-start | bytes 6148
  104.8 2.9 %copy-start.1 = (bf16[1,91,1,8,1024]{1,4,3,2,0:T(8,128)(2,1)S(1)}, bf16[1,91,1,8,1024]{1,4,3,2,0:T(8,128)(2,1)}, u32[]{:S(2)}) copy-start(bf16[1,91,1,8,1024]{1,4,3,2,0:T(8,128)(2,1)} %copy.11) | copy-start | bytes 4472836
Sparse Core Ops, SparseCore 0:
  8.9 31.8 all-gather.3
  42.4 47.9 all-gather.5
  92.1 27.3 all-gather.7
